TPU v7x, 32 devices: a whole 2x2x4 slice. The times are simulated.
32 devices in a mesh: expert: 16 (over z, y, x), tensor: 2 (over core).
Axes of the slice: x: 2, y: 2, z: 4, core: 2. Of those that a mesh axis runs over, the one named last changes fastest.
Arguments:
- grad_out: bfloat16 [256, 3584], P('expert'), may hold values from -1.5 to 1.5
- expert_ids: int32 [256, 8], P('expert'), may hold values from 0 to 15, all different within a row; in each aligned block of 16 rows (0 to 15, 16 to 31, ...) at most 16 rows name the same one
- gate_values: float32 [256, 8], P('expert'), may hold values from 0.05 to 0.6
- w_gate_up: bfloat16 [16, 2, 3584, 1024], P('expert', None, None, 'tensor'), may hold values from -0.09375 to 0.09375
- w_down: bfloat16 [16, 1024, 3584], P('expert', 'tensor'), may hold values from -0.1875 to 0.1875
- saved_routed: bfloat16 [16, 2, 256, 1024], P('expert', None, None, 'tensor'), may hold values from -6 to 6
- shared_gate_up: bfloat16 [2, 3584, 1024], P(None, 'expert', 'tensor'), may hold values from -0.09375 to 0.09375
- shared_down: bfloat16 [1024, 3584], P('tensor', 'expert'), may hold values from -0.1875 to 0.1875
- saved_shared: bfloat16 [2, 256, 1024], P(None, 'expert', 'tensor'), may hold values from -6 to 6
Outputs:
- grad_in: bfloat16 [256, 3584], P('expert', 'tensor')
- grad_gates: float32 [256, 8], P('expert')
Inputs may be any that keep to these rules, and one draw needn't show every extreme that they name: `expert_ids`: each row names 8 different experts. Among the 16 rows of one index of expert (aligned blocks of rows), no expert is named by more than 16 rows, and in some block one expert is named by exactly 16 rows.
All inputs are finite; a program needn't handle non-finite values.
Results may differ from a plain program's by a relative error of at most 0.015.
Values may be sent and summed in bfloat16 or wider, within the bound.
A program may use at most 64 MiB of HBM per device.

v0:
```python
import jax
import jax.numpy as jnp
from jax import lax
from jax.sharding import PartitionSpec as P


def contract_last(left_side, right_side):
    return lax.dot_general(
        left_side, right_side, (((1,), (1,)), ((), ())), preferred_element_type=jnp.float32
    )


def swiglu_grads(back_grad, saved_gate, saved_up):
    pre_gate = saved_gate.astype(jnp.float32)
    pre_up = saved_up.astype(jnp.float32)
    sigmoid = jax.nn.sigmoid(pre_gate)
    grad_gate = (back_grad * pre_up * sigmoid * (1.0 + pre_gate * (1.0 - sigmoid))).astype(
        jnp.bfloat16
    )
    grad_up = (back_grad * pre_gate * sigmoid).astype(jnp.bfloat16)
    return (grad_gate, grad_up)


def gate_mixture(back_grad, saved_gate, saved_up):
    pre_gate = saved_gate.astype(jnp.float32)
    pre_up = saved_up.astype(jnp.float32)
    sigmoid = jax.nn.sigmoid(pre_gate)
    return back_grad * pre_gate * sigmoid * pre_up


def per_device(
    grad_out,
    expert_ids,
    gate_values,
    w_gate_up,
    w_down,
    saved_routed,
    shared_gate_up,
    shared_down,
    saved_shared,
):
    experts = lax.axis_size("expert")
    tokens, features = grad_out.shape
    choose = expert_ids.shape[1]
    slot_count = saved_routed.shape[2]
    capacity = slot_count // experts
    flat_ids = expert_ids.reshape(-1)
    onehot = (flat_ids[:, None] == jnp.arange(experts, dtype=jnp.int32)[None, :]).astype(jnp.int32)
    earlier = jnp.cumsum(onehot, axis=0) - onehot
    position = jnp.sum(earlier * onehot, axis=1)
    slot_index = flat_ids * capacity + position
    pair_token = jnp.arange(tokens * choose, dtype=jnp.int32) // choose
    source_row = jnp.full((slot_count,), tokens, jnp.int32).at[slot_index].set(pair_token)
    padded = jnp.concatenate([grad_out, jnp.zeros((1, features), grad_out.dtype)], axis=0)
    send_rows = padded[source_row].reshape(experts, capacity, features)
    arrived = lax.all_to_all(send_rows, "expert", split_axis=0, concat_axis=0, tiled=True)
    slot_rows = arrived.reshape(slot_count, features)
    back_grad = contract_last(slot_rows, w_down[0])
    grad_gate, grad_up = swiglu_grads(back_grad, saved_routed[0, 0], saved_routed[0, 1])
    gate_mix = gate_mixture(back_grad, saved_routed[0, 0], saved_routed[0, 1])
    row_terms = contract_last(grad_gate, w_gate_up[0, 0]) + contract_last(grad_up, w_gate_up[0, 1])
    gate_terms = jnp.sum(gate_mix, axis=1).astype(jnp.bfloat16)
    shared_back = contract_last(grad_out, lax.all_gather(shared_down, "expert", axis=1, tiled=True))
    shared_gate, shared_up = swiglu_grads(shared_back, saved_shared[0], saved_shared[1])
    weight_piece = lax.all_gather(shared_gate_up, "expert", axis=1, tiled=True)
    shared_term = contract_last(shared_gate, weight_piece[0]) + contract_last(
        shared_up, weight_piece[1]
    )
    outgoing = row_terms.astype(jnp.bfloat16).reshape(experts, capacity, features)
    returned, gate_back = (
        lax.all_to_all(outgoing, "expert", split_axis=0, concat_axis=0, tiled=True),
        lax.all_to_all(
            gate_terms.reshape(experts, capacity), "expert", split_axis=0, concat_axis=0, tiled=True
        ),
    )
    picked = returned.reshape(slot_count, features)[slot_index].reshape(tokens, choose, features)
    routed = jnp.einsum("tkd,tk->td", picked.astype(jnp.float32), gate_values)
    summed = lax.psum_scatter(
        (routed + shared_term).astype(jnp.bfloat16), "tensor", scatter_dimension=1, tiled=True
    )
    gate_pairs = (
        gate_back.reshape(slot_count)[slot_index].reshape(tokens, choose).astype(jnp.float32)
    )
    grad_gates = lax.psum(gate_pairs, "tensor")
    return (summed, grad_gates)


def solution(mesh):
    return jax.shard_map(
        per_device,
        mesh=mesh,
        in_specs=(
            P("expert", None),
            P("expert", None),
            P("expert", None),
            P("expert", None, None, "tensor"),
            P("expert", "tensor", None),
            P("expert", None, None, "tensor"),
            P(None, "expert", "tensor"),
            P("tensor", "expert"),
            P(None, "expert", "tensor"),
        ),
        out_specs=(P("expert", "tensor"), P("expert", None)),
        check_vma=False,
    )
```

profile of v0, /device:TPU:0, one launch (start us, length us, event | category | flops | bytes accessed | tf_op | source)
XLA Modules:
  0.0 253.5 jit_solution(2283505379111606184)
XLA Ops:
  7.2 0.7 all-gather.3.cloned.1.call-update
  7.9 0.7 all-gather.5.cloned.1.call-update
  8.6 0.8 copy.18
  9.4 0.1 eq.15
  9.5 0.7 broadcast_multiply_fusion
  10.3 0.1 mul.62
  10.4 0.1 fusion.29
  10.4 0.2 reduce_window_sum.11
  10.6 0.9 concatenate.3
  11.5 0.2 select_reduce_fusion
  11.7 1.0 scatter_custom_fusion
  12.8 1.7 gather_fusion
  14.5 66.9 %all_to_all.16 = bf16[16,16,3584]{2,1,0:T(8,128)(2,1)S(1)} all-to-all(bf16[16,16,3584]{2,1,0:T(8,128)(2,1)S(1)} %bitcast.73), channel_id=1, replica_groups=mesh['expert'=16,'tensor'=2] {'expert'}, dimensions={0} | all-to-all | bytes 3670016 | tf_op jit(solution)/shard_map/all_to_all | solution.py:56
  81.4 1.3 fusion.16
  82.7 3.4 %fusion.5 = f32[256,3584]{1,0:T(8,128)S(1)} fusion(bf16[1,2,3584,512]{3,2,1,0:T(8,128)(2,1)} %param.12, f32[256,512]{1,0:T(8,128)S(1)} %get-tuple-element.9, bf16[1,2,256,512]{3,2,1,0:T(8,128)(2,1)S(1)} %copy-done.4), kind=kOutput, calls=%fused_computation.13 | convolution fusion | flops 941096960 | bytes 8388608 | tf_op jit(solution)/shard_map/dot_general | solution.py:8
  86.2 2.4 fusion
  88.6 7.1 %all-to-all-start.1 = ((bf16[16,16,3584]{2,1,0:T(8,128)(2,1)}), bf16[16,16,3584]{2,1,0:T(8,128)(2,1)S(1)}, u32[]{:S(2)}, u32[]{:S(2)}) async-start(bf16[16,16,3584]{2,1,0:T(8,128)(2,1)} %bitcast.74), calls=%async_computation.1 | async-start | bytes 3670016 | tf_op jit(solution)/shard_map/all_to_all | solution.py:71
  95.8 0.1 copy.21
  95.9 47.3 %all-to-all-done.1 = bf16[16,16,3584]{2,1,0:T(8,128)(2,1)S(1)} async-done(((bf16[16,16,3584]{2,1,0:T(8,128)(2,1)}), bf16[16,16,3584]{2,1,0:T(8,128)(2,1)S(1)}, u32[]{:S(2)}, u32[]{:S(2)}) %all-to-all-start.1) | async-done | bytes 1835040 | tf_op jit(solution)/shard_map/all_to_all | solution.py:71
  143.2 1.1 gather_fusion.1
  144.4 0.4 fusion.11
  144.8 2.6 %fusion.56 = f32[16,512]{1,0:T(8,128)S(1)} fusion(bf16[16,3584]{1,0:T(8,128)(2,1)S(1)} %copy-done, bf16[512,3584]{0,1:T(8,128)(2,1)} %all-gather.3.cloned.1.call-done), kind=kOutput, calls=%fused_computation.81 | convolution fusion | flops 58720256 | bytes 3817472 | tf_op jit(solution)/shard_map/dot_general | solution.py:8
  147.4 76.9 %all-gather.5.cloned.1.call-done = bf16[2,3584,512]{2,1,0:T(8,128)(2,1)} async-done(((bf16[2,224,512]{2,1,0:T(8,128)(2,1)}), bf16[2,3584,512]{2,1,0:T(8,128)(2,1)}) %all-gather.5.cloned.1.call-update) | async-done | bytes 7340048 | tf_op jit(solution)/shard_map/all_gather | solution.py:65
  224.3 3.1 %fusion.3 = f32[16,3584]{1,0:T(8,128)S(1)} fusion(bf16[2,3584,512]{2,1,0:T(8,128)(2,1)} %all-gather.5.cloned.1.call-done, f32[16,512]{1,0:T(8,128)S(1)} %fusion.56, bf16[2,16,512]{2,1,0:T(8,128)(2,1)S(1)} %copy-done.1), kind=kOutput, calls=%fused_computation.11 | convolution fusion | flops 58818560 | bytes 3964928 | tf_op jit(solution)/shard_map/dot_general | solution.py:8
  227.4 3.8 %fusion.2 = bf16[16,3584]{1,0:T(8,128)(2,1)} fusion(f32[16,3584]{1,0:T(8,128)S(1)} %fusion.3, bf16[2,3584,512]{2,1,0:T(8,128)(2,1)} %all-gather.5.cloned.1.call-done, f32[16,1,3584]{2,1,0:T(1,128)S(1)} %fusion.11, f32[16,512]{1,0:T(8,128)S(1)} %fusion.56, bf16[2,16,512]{2,1,0:T(8,128)(2,1)S(1)} %copy-done.1), kind=kOutput, calls=%fused_computation.8 | convolution fusion | flops 58949632 | bytes 4292608 | tf_op jit(solution)/shard_map/dot_general | solution.py:8
  231.2 0.1 convert_element_type.92
  231.3 11.1 %all_to_all.17 = bf16[16,1,16]{2,1,0:T(2,128)(2,1)S(1)} all-to-all(bf16[16,1,16]{2,1,0:T(2,128)(2,1)S(1)} %convert_element_type.92), channel_id=1, replica_groups=mesh['expert'=16,'tensor'=2] {'expert'}, dimensions={0} | all-to-all | bytes 1024 | tf_op jit(solution)/shard_map/all_to_all | solution.py:72
  242.4 0.1 reshape.84
  242.5 1.2 gather_fusion.2
  243.7 0.1 reshape.89
  243.8 2.5 psum.7
  246.3 0.7 copy.20
  (28 shorter events, 0.3 us)
Async XLA Ops:
  7.2 137.6 %all-gather.3.cloned.1.call-start = ((), (), s32[]{:S(2)}) async-start(), calls=%async_computation.4 | async-start | bytes 3899392 | tf_op jit(solution)/shard_map/all_gather | solution.py:63
  7.9 216.4 %all-gather.5.cloned.1.call-start = ((), (), s32[]{:S(2)}) async-start(), calls=%async_computation.5 | async-start | bytes 7798784 | tf_op jit(solution)/shard_map/all_gather | solution.py:65
  12.7 68.7 %copy-start.4 = (bf16[1,2,256,512]{3,2,1,0:T(8,128)(2,1)S(1)}, bf16[1,2,256,512]{3,2,1,0:T(8,128)(2,1)}, u32[]{:S(2)}) copy-start(bf16[1,2,256,512]{3,2,1,0:T(8,128)(2,1)} %param.14) | copy-start | bytes 1572868
  14.5 66.9 %copy-start.3 = (bf16[1,512,3584]{2,1,0:T(8,128)(2,1)S(1)}, bf16[1,512,3584]{2,1,0:T(8,128)(2,1)}, u32[]{:S(2)}) copy-start(bf16[1,512,3584]{2,1,0:T(8,128)(2,1)} %param.13) | copy-start | bytes 11010052
  81.4 4.8 %slice-start = ((s8[7340032]{0:T(1024)(128)(4,1)}), s8[4194304]{0:T(1024)(128)(4,1)S(1)}, s32[]{:S(2)}) async-start(s8[7340032]{0:T(1024)(128)(4,1)} %bitcast.77), calls=%async_computation.7 | async-start | bytes 8388608
  82.7 3.5 %slice-start.1 = ((s8[7340032]{0:T(1024)(128)(4,1)}), s8[3145728]{0:T(1024)(128)(4,1)S(1)}, s32[]{:S(2)}) async-start(s8[7340032]{0:T(1024)(128)(4,1)} %bitcast.77), calls=%async_computation.8 | async-start | bytes 6291456
  88.6 7.2 %copy-start.2 = (f32[16,8]{0,1:T(8,128)S(1)}, f32[16,8]{0,1:T(8,128)}, u32[]{:S(2)}) copy-start(f32[16,8]{0,1:T(8,128)} %param.11) | copy-start | bytes 1540
  88.6 54.6 %all-to-all-start.1 = ((bf16[16,16,3584]{2,1,0:T(8,128)(2,1)}), bf16[16,16,3584]{2,1,0:T(8,128)(2,1)S(1)}, u32[]{:S(2)}, u32[]{:S(2)}) async-start(bf16[16,16,3584]{2,1,0:T(8,128)(2,1)} %bitcast.74), calls=%async_computation.1 | async-start | bytes 3670016 | tf_op jit(solution)/shard_map/all_to_all | solution.py:71
  95.8 151.2 %reduce-scatter.2.cloned.1.call-start = ((), (), s32[]{:S(2)}) async-start(), calls=%async_computation.6 | async-start | bytes 172032 | tf_op jit(solution)/shard_map/reduce_scatter | solution.py:78
  143.2 1.6 copy-start
  144.4 79.9 %copy-start.1 = (bf16[2,16,512]{2,1,0:T(8,128)(2,1)S(1)}, bf16[2,16,512]{2,1,0:T(8,128)(2,1)}, u32[]{:S(2)}) copy-start(bf16[2,16,512]{2,1,0:T(8,128)(2,1)} %param.17) | copy-start | bytes 98308
Sparse Core Ops, SparseCore 0:
  10.7 103.8 all-gather.2
  117.3 106.9 all-gather.4
  231.3 5.9 reduce-scatter.1
where the time goes:
time: 254 us; the launch traced here: 253 us
  waiting for transfers between devices  126 us (50%)
  blocking collectives  80.5 us (32%)
  matrix products  17 us (7%)
  between operations  13.9 us (5%)
  local copies, waits for them, and re-layouts  8 us (3%)
  starting transfers between devices  7.26 us (3%)
    all_gather x1, waiting for transfers between devices, per_device(): weight_piece = lax.all_gather(shared_gate_up, 'expert', axis=1, tiled=True)  76.9 us
    all_to_all x1, blocking collectives, per_device(): lax.all_to_all(send_rows, 'expert', split_axis=0, concat_axis=0, tiled=True)  66.9 us
    all_to_all x1, waiting for transfers between devices, per_device(): lax.all_to_all(outgoing, 'expert', split_axis=0, concat_axis=0, tiled=True)  47.3 us
    dot_general x6, matrix products, contract_last(): lax.dot_general(left_side, right_side, (((1,), (1,)), ((), ())), preferre...  16.7 us
    all_to_all x1, blocking collectives, per_device(): lax.all_to_all(gate_terms.reshape(experts, capacity), 'expert', split_axi...  11.1 us
    all_to_all x1, starting transfers between devices, per_device(): lax.all_to_all(outgoing, 'expert', split_axis=0, concat_axis=0, tiled=True)  7.14 us
  transfers between devices with their start and end apart: 4, of which 2 were waited for; matrix products, arithmetic and copies ran while one was open for 8% of the time, Pallas kernels for 0%

commit v1 on v0

--- a/solution.py
+++ b/solution.py
@@ -62,7 +62,7 @@
     gate_terms = jnp.sum(gate_mix, axis=1).astype(jnp.bfloat16)
     shared_back = contract_last(grad_out, lax.all_gather(shared_down, "expert", axis=1, tiled=True))
     shared_gate, shared_up = swiglu_grads(shared_back, saved_shared[0], saved_shared[1])
-    weight_piece = lax.all_gather(shared_gate_up, "expert", axis=1, tiled=True)
+    weight_piece = jnp.concatenate(jax.lax.all_gather(shared_gate_up, "expert"), axis=1)
     shared_term = contract_last(shared_gate, weight_piece[0]) + contract_last(
         shared_up, weight_piece[1]
     )

time: 254 us -> 254 us (level)
  matrix products: 17 us -> 12.9 us
  local copies, waits for them, and re-layouts: 8 us -> 12 us
    dot_general x6, matrix products: 16.7 us -> 12.6 us  [contract_last(): lax.dot_general(left_side, right_side, (((1,), (1,)), ((), ())), preferre...]
    slice x0 -> x1, local copies, waits for them, and re-layouts: none -> 3.96 us  [per_device(): weight_piece[1]]
where the time goes in v1:
time: 254 us; the launch traced here: 253 us
  waiting for transfers between devices  126 us (50%)
  blocking collectives  80.4 us (32%)
  between operations  13.9 us (5%)
  matrix products  12.9 us (5%)
  local copies, waits for them, and re-layouts  12 us (5%)
  starting transfers between devices  7.26 us (3%)
    all_gather x1, waiting for transfers between devices, per_device(): jax.lax.all_gather(shared_gate_up, 'expert')  76.8 us
    all_to_all x1, blocking collectives, per_device(): lax.all_to_all(send_rows, 'expert', split_axis=0, concat_axis=0, tiled=True)  66.9 us
    all_to_all x1, waiting for transfers between devices, per_device(): lax.all_to_all(outgoing, 'expert', split_axis=0, concat_axis=0, tiled=True)  47.4 us
    dot_general x6, matrix products, contract_last(): lax.dot_general(left_side, right_side, (((1,), (1,)), ((), ())), preferre...  12.6 us
    all_to_all x1, blocking collectives, per_device(): lax.all_to_all(gate_terms.reshape(experts, capacity), 'expert', split_axi...  11 us
    all_to_all x1, starting transfers between devices, per_device(): lax.all_to_all(outgoing, 'expert', split_axis=0, concat_axis=0, tiled=True)  7.14 us
  transfers between devices with their start and end apart: 4, of which 2 were waited for; matrix products, arithmetic and copies ran while one was open for 8% of the time, Pallas kernels for 0%

profile of v1, /device:TPU:0, one launch (start us, length us, event | category | flops | bytes accessed | tf_op | source)
XLA Modules:
  0.0 253.4 jit_solution(10387775928016344583)
XLA Ops:
  7.2 0.7 all-gather.4.cloned.1.call-update
  7.9 0.7 all-gather.6.cloned.1.call-update
  8.6 0.8 copy.18
  9.4 0.7 broadcast_multiply_fusion
  10.2 0.1 mul.62
  10.3 0.1 eq.15
  10.3 0.1 fusion.28
  10.4 0.2 reduce_window_sum.11
  10.6 0.9 concatenate.3
  11.5 0.2 select_reduce_fusion
  11.7 1.0 scatter_custom_fusion
  12.8 1.7 gather_fusion
  14.5 66.9 %all_to_all.16 = bf16[16,16,3584]{2,1,0:T(8,128)(2,1)S(1)} all-to-all(bf16[16,16,3584]{2,1,0:T(8,128)(2,1)S(1)} %bitcast.77), channel_id=1, replica_groups=mesh['expert'=16,'tensor'=2] {'expert'}, dimensions={0} | all-to-all | bytes 3670016 | tf_op jit(solution)/shard_map/all_to_all | solution.py:56
  81.4 1.3 fusion.15
  82.7 3.4 %fusion.4 = f32[256,3584]{1,0:T(8,128)S(1)} fusion(bf16[1,2,3584,512]{3,2,1,0:T(8,128)(2,1)} %param.12, f32[256,512]{1,0:T(8,128)S(1)} %get-tuple-element.11, bf16[1,2,256,512]{3,2,1,0:T(8,128)(2,1)S(1)} %copy-done.4), kind=kOutput, calls=%fused_computation.10 | convolution fusion | flops 941096960 | bytes 8388608 | tf_op jit(solution)/shard_map/dot_general | solution.py:8
  86.2 2.4 fusion
  88.6 7.1 %all-to-all-start.1 = ((bf16[16,16,3584]{2,1,0:T(8,128)(2,1)}), bf16[16,16,3584]{2,1,0:T(8,128)(2,1)S(1)}, u32[]{:S(2)}, u32[]{:S(2)}) async-start(bf16[16,16,3584]{2,1,0:T(8,128)(2,1)} %bitcast.79), calls=%async_computation.1 | async-start | bytes 3670016 | tf_op jit(solution)/shard_map/all_to_all | solution.py:71
  95.9 47.4 %all-to-all-done.1 = bf16[16,16,3584]{2,1,0:T(8,128)(2,1)S(1)} async-done(((bf16[16,16,3584]{2,1,0:T(8,128)(2,1)}), bf16[16,16,3584]{2,1,0:T(8,128)(2,1)S(1)}, u32[]{:S(2)}, u32[]{:S(2)}) %all-to-all-start.1) | async-done | bytes 1835040 | tf_op jit(solution)/shard_map/all_to_all | solution.py:71
  143.3 1.1 gather_fusion.1
  144.5 0.4 fusion.10
  144.9 2.6 %fusion.57 = f32[16,512]{1,0:T(8,128)S(1)} fusion(bf16[16,3584]{1,0:T(8,128)(2,1)S(1)} %copy-done, bf16[512,3584]{0,1:T(8,128)(2,1)} %all-gather.4.cloned.1.call-done), kind=kOutput, calls=%fused_computation.80 | convolution fusion | flops 58720256 | bytes 3817472 | tf_op jit(solution)/shard_map/dot_general | solution.py:8
  147.5 76.8 %all-gather.6.cloned.1.call-done = bf16[32,224,512]{2,1,0:T(8,128)(2,1)} async-done(((bf16[2,224,512]{2,1,0:T(8,128)(2,1)}), bf16[32,224,512]{2,1,0:T(8,128)(2,1)}) %all-gather.6.cloned.1.call-update) | async-done | bytes 7340048 | tf_op jit(solution)/shard_map/all_gather | solution.py:65
  224.3 4.0 %fusion.56 = (bf16[1,16,224,512]{3,2,0,1:T(8,128)(2,1)S(1)}, bf16[1,16,224,512]{3,2,0,1:T(8,128)(2,1)S(1)}) fusion(bf16[2,16,224,512]{3,2,0,1:T(8,128)(2,1)} %bitcast.78), kind=kLoop, calls=%fused_computation.79 | loop fusion | bytes 14680064 | tf_op jit(solution)/shard_map/slice | solution.py:67
  228.3 1.1 fusion.39
  229.4 1.7 fusion.2
  231.1 0.1 convert_element_type.92
  231.2 11.0 %all_to_all.17 = bf16[16,1,16]{2,1,0:T(2,128)(2,1)S(1)} all-to-all(bf16[16,1,16]{2,1,0:T(2,128)(2,1)S(1)} %convert_element_type.92), channel_id=1, replica_groups=mesh['expert'=16,'tensor'=2] {'expert'}, dimensions={0} | all-to-all | bytes 1024 | tf_op jit(solution)/shard_map/all_to_all | solution.py:72
  242.3 0.1 reshape.93
  242.4 1.2 gather_fusion.2
  243.6 0.1 reshape.98
  243.7 2.5 psum.7
  246.2 0.7 copy.20
  (29 shorter events, 0.4 us)
Async XLA Ops:
  7.2 137.7 %all-gather.4.cloned.1.call-start = ((), (), s32[]{:S(2)}) async-start(), calls=%async_computation.4 | async-start | bytes 3899392 | tf_op jit(solution)/shard_map/all_gather | solution.py:63
  7.9 216.4 %all-gather.6.cloned.1.call-start = ((), (), s32[]{:S(2)}) async-start(), calls=%async_computation.6 | async-start | bytes 7798784 | tf_op jit(solution)/shard_map/all_gather | solution.py:65
  12.7 68.7 %copy-start.4 = (bf16[1,2,256,512]{3,2,1,0:T(8,128)(2,1)S(1)}, bf16[1,2,256,512]{3,2,1,0:T(8,128)(2,1)}, u32[]{:S(2)}) copy-start(bf16[1,2,256,512]{3,2,1,0:T(8,128)(2,1)} %param.14) | copy-start | bytes 1572868
  14.5 66.9 %copy-start.3 = (bf16[1,512,3584]{2,1,0:T(8,128)(2,1)S(1)}, bf16[1,512,3584]{2,1,0:T(8,128)(2,1)}, u32[]{:S(2)}) copy-start(bf16[1,512,3584]{2,1,0:T(8,128)(2,1)} %param.13) | copy-start | bytes 11010052
  81.4 4.8 %slice-start = ((s8[7340032]{0:T(1024)(128)(4,1)}), s8[4194304]{0:T(1024)(128)(4,1)S(1)}, s32[]{:S(2)}) async-start(s8[7340032]{0:T(1024)(128)(4,1)} %bitcast.82), calls=%async_computation.7 | async-start | bytes 8388608
  82.7 3.5 %slice-start.1 = ((s8[7340032]{0:T(1024)(128)(4,1)}), s8[3145728]{0:T(1024)(128)(4,1)S(1)}, s32[]{:S(2)}) async-start(s8[7340032]{0:T(1024)(128)(4,1)} %bitcast.82), calls=%async_computation.8 | async-start | bytes 6291456
  88.6 7.2 %copy-start.2 = (f32[16,8]{0,1:T(8,128)S(1)}, f32[16,8]{0,1:T(8,128)}, u32[]{:S(2)}) copy-start(f32[16,8]{0,1:T(8,128)} %param.11) | copy-start | bytes 1540
  88.6 54.7 %all-to-all-start.1 = ((bf16[16,16,3584]{2,1,0:T(8,128)(2,1)}), bf16[16,16,3584]{2,1,0:T(8,128)(2,1)S(1)}, u32[]{:S(2)}, u32[]{:S(2)}) async-start(bf16[16,16,3584]{2,1,0:T(8,128)(2,1)} %bitcast.79), calls=%async_computation.1 | async-start | bytes 3670016 | tf_op jit(solution)/shard_map/all_to_all | solution.py:71
  95.8 151.1 %reduce-scatter.2.cloned.1.call-start = ((), (), s32[]{:S(2)}) async-start(), calls=%async_computation.5 | async-start | bytes 172032 | tf_op jit(solution)/shard_map/reduce_scatter | solution.py:78
  143.3 1.5 copy-start
  224.3 4.0 %copy-start.1 = (bf16[2,16,512]{2,1,0:T(8,128)(2,1)S(1)}, bf16[2,16,512]{2,1,0:T(8,128)(2,1)}, u32[]{:S(2)}) copy-start(bf16[2,16,512]{2,1,0:T(8,128)(2,1)} %param.17) | copy-start | bytes 98308
Sparse Core Ops, SparseCore 0:
  10.7 103.8 all-gather.3
  117.3 107.0 all-gather.5
  231.2 5.8 reduce-scatter.1
